TPU v7x, 32 devices: a whole 2x2x4 slice. The times are simulated.
32 devices in a mesh: sy: 4 (over y, x), sx: 4 (over z), wl: 2 (over core).
Axes of the slice: x: 2, y: 2, z: 4, core: 2. Of those that a mesh axis runs over, the one named last changes fastest.
Arguments:
- interface_map: bfloat16 [8, 4, 1536, 2, 1536], P(('wl', 'sy'), 'sx'), parts along dimension 0, may hold values from -0.0625 to 0.0625
- source_trace: float32 [8, 4, 2, 64, 4, 384], P(('wl', 'sy'), 'sx'), parts along dimension 0, may hold values from -6 to 6
- restriction: float32 [8, 4, 2, 32, 4, 384], P(('wl', 'sy'), 'sx'), parts along dimension 0, may hold values from -0.02734375 to 0.02734375
- prolongation: float32 [8, 4, 2, 32, 4, 384], P(('wl', 'sy'), 'sx'), parts along dimension 0, may hold values from -0.109375 to 0.109375
- coarse_inverse: float32 [4, 32, 32], P('wl'), parts along dimension 0, may hold values from -0.75 to 0.75
Outputs:
- traces: float32 [8, 4, 2, 64, 4, 384], P(('wl', 'sy'), 'sx'), parts along dimension 0
- coarse_coef: float32 [4, 64, 32], P('wl'), parts along dimension 0
There are 2 independent parts, one for each index of `wl`. A program takes and returns all parts, laid end to end along the dimension named above; each array names one. Nothing has to cross between parts.
All inputs are finite; a program needn't handle non-finite values.
Results may differ from a plain program's by a relative error of at most 0.0025.
Values sent between devices are 32-bit elements; how exact they have to be, the bound alone decides.
A program may use at most 128 MiB of HBM per device.

v0:
```python
import jax
import jax.numpy as jnp
from jax import lax
from jax.sharding import PartitionSpec as P

ITERS = 6


PRECISE = lax.Precision.HIGHEST


def shifted(value, axis, by):
    peers = lax.axis_size(axis)
    pairs = [(i, i + by) for i in range(peers) if 0 <= i + by < peers]
    return lax.ppermute(value, axis, pairs)


def with_halo(value, sides, width):
    for axis, dim in sides:
        peers, length = (lax.axis_size(axis), value.shape[dim])
        up = [(i, (i + 1) % peers) for i in range(peers - 1)]
        down = [(j, i) for i, j in up]
        last = lax.slice_in_dim(value, length - width, length, axis=dim)
        initial = lax.slice_in_dim(value, 0, width, axis=dim)
        before = lax.ppermute(last, axis, up)
        after = lax.ppermute(initial, axis, down)
        value = jnp.concatenate([before, value, after], axis=dim)
    return value


def complex_pair(left_real, left_imag, right_real, right_imag, pattern):
    real_part = jnp.einsum(pattern, left_real, right_real, precision=PRECISE) - jnp.einsum(
        pattern, left_imag, right_imag, precision=PRECISE
    )
    imag_part = jnp.einsum(pattern, left_real, right_imag, precision=PRECISE) + jnp.einsum(
        pattern, left_imag, right_real, precision=PRECISE
    )
    return jnp.stack([real_part, imag_part])


def corner_values(outgoing):
    corner_northwest = outgoing[..., 0, 0] + outgoing[..., 2, 0]
    corner_northeast = outgoing[..., 0, -1] + outgoing[..., 3, 0]
    corner_southwest = outgoing[..., 1, 0] + outgoing[..., 2, -1]
    corner_southeast = outgoing[..., 1, -1] + outgoing[..., 3, -1]
    return (corner_northwest, corner_northeast, corner_southwest, corner_southeast)


def assemble(
    from_north,
    from_south,
    from_west,
    from_east,
    into_northwest,
    into_northeast,
    into_southwest,
    into_southeast,
):
    north_side = (
        from_north.at[..., 0].add(0.5 * into_northwest).at[..., -1].add(0.5 * into_northeast)
    )
    south_side = (
        from_south.at[..., 0].add(0.5 * into_southwest).at[..., -1].add(0.5 * into_southeast)
    )
    west_side = from_west.at[..., 0].add(0.5 * into_northwest).at[..., -1].add(0.5 * into_southwest)
    east_side = from_east.at[..., 0].add(0.5 * into_northeast).at[..., -1].add(0.5 * into_southeast)
    return jnp.stack([north_side, south_side, west_side, east_side], axis=-2)


def restrict_sum(traces, weights):
    src_count, side_len = (traces.shape[1], traces.shape[3])
    coarse_width = weights.shape[1]
    flat_traces = traces.reshape(2, src_count, 4 * side_len)
    flat_weights = weights.reshape(2, coarse_width, 4 * side_len)
    return complex_pair(
        flat_traces[0], flat_traces[1], flat_weights[0], flat_weights[1], "sk,nk->sn"
    )


def outgoing_traces(traces, map_shard, source_shard):
    src_count, side_len = (traces.shape[1], traces.shape[3])
    row_block = traces.astype(jnp.bfloat16).reshape(2 * src_count, 4 * side_len)
    map_table = map_shard.reshape(4 * side_len, 8 * side_len)
    product = jnp.dot(row_block, map_table, preferred_element_type=jnp.float32).reshape(
        2, src_count, 2, 4 * side_len
    )
    real_part = product[0, :, 0] - product[1, :, 1]
    imag_part = product[0, :, 1] + product[1, :, 0]
    return jnp.stack([real_part, imag_part]).reshape(2, src_count, 4, side_len) + source_shard


def exchange_direct(outgoing):
    from_north = shifted(outgoing[:, :, 1], "sy", 1)
    from_south = shifted(outgoing[:, :, 0], "sy", -1)
    from_west = shifted(outgoing[:, :, 3], "sx", 1)
    from_east = shifted(outgoing[:, :, 2], "sx", -1)
    corner_northwest, corner_northeast, corner_southwest, corner_southeast = corner_values(outgoing)
    corner_grid = jnp.stack(
        [
            jnp.stack([corner_northwest, corner_northeast]),
            jnp.stack([corner_southwest, corner_southeast]),
        ]
    )
    padded = with_halo(corner_grid, (("sy", 0), ("sx", 1)), 1)
    return assemble(
        from_north,
        from_south,
        from_west,
        from_east,
        padded[0, 0],
        padded[0, 3],
        padded[3, 0],
        padded[3, 3],
    )


def sender_restriction(weights):
    receive_northwest = 0.5 * (weights[:, :, 0, 0] + weights[:, :, 2, 0])
    receive_northeast = 0.5 * (weights[:, :, 0, -1] + weights[:, :, 3, 0])
    receive_southwest = 0.5 * (weights[:, :, 1, 0] + weights[:, :, 2, -1])
    receive_southeast = 0.5 * (weights[:, :, 1, -1] + weights[:, :, 3, -1])
    empty_slot = jnp.zeros_like(weights[:, :, 0])

    def spread_slot(vector):
        return jnp.broadcast_to(vector[:, :, None], empty_slot.shape)

    weight_grid = jnp.stack(
        [
            jnp.stack(
                [spread_slot(receive_northwest), weights[:, :, 0], spread_slot(receive_northeast)]
            ),
            jnp.stack([weights[:, :, 2], empty_slot, weights[:, :, 3]]),
            jnp.stack(
                [spread_slot(receive_southwest), weights[:, :, 1], spread_slot(receive_southeast)]
            ),
        ]
    )
    padded = with_halo(weight_grid, (("sy", 0), ("sx", 1)), 1)
    weight_northwest = padded[0, 0][..., 0]
    weight_northeast = padded[0, 4][..., 0]
    weight_southwest = padded[4, 0][..., 0]
    weight_southeast = padded[4, 4][..., 0]
    north_weights = padded[0, 2].at[..., 0].add(weight_northwest).at[..., -1].add(weight_northeast)
    south_weights = padded[4, 2].at[..., 0].add(weight_southwest).at[..., -1].add(weight_southeast)
    west_weights = padded[2, 0].at[..., 0].add(weight_northwest).at[..., -1].add(weight_southwest)
    east_weights = padded[2, 4].at[..., 0].add(weight_northeast).at[..., -1].add(weight_southeast)
    return jnp.stack([north_weights, south_weights, west_weights, east_weights], axis=2)


def per_device(interface_map, source_trace, restriction, prolongation, coarse_inverse):
    source_shard = source_trace[0, 0]
    weights = restriction[0, 0]
    src_count, side_len = (source_shard.shape[1], source_shard.shape[3])
    coarse_width = weights.shape[1]
    lift_flat = prolongation[0, 0].reshape(2, coarse_width, 4 * side_len)
    traces = jnp.zeros(source_shard.shape, jnp.float32)
    coef_now = jnp.zeros((2, src_count, coarse_width), jnp.float32)
    coarse_total = coef_now
    sender_weights = sender_restriction(weights)
    for sweep_index in range(ITERS):
        coef_now = complex_pair(
            coarse_total[0], coarse_total[1], coarse_inverse[0], coarse_inverse[1], "sn,nq->sq"
        )
        spread = complex_pair(coef_now[0], coef_now[1], lift_flat[0], lift_flat[1], "sn,nk->sk")
        corrected = traces + spread.reshape(traces.shape)
        outgoing = outgoing_traces(corrected, interface_map, source_shard)
        if sweep_index + 1 < ITERS:
            coarse_total = lax.psum(restrict_sum(outgoing, sender_weights), ("sy", "sx"))
        traces = exchange_direct(outgoing)
    return (traces[None, None], coef_now)


def solution(mesh):
    return jax.shard_map(
        per_device,
        mesh=mesh,
        in_specs=(
            P(("wl", "sy"), "sx", None, None, None),
            P(("wl", "sy"), "sx", None, None, None, None),
            P(("wl", "sy"), "sx", None, None, None, None),
            P(("wl", "sy"), "sx", None, None, None, None),
            P("wl", None, None),
        ),
        out_specs=(P(("wl", "sy"), "sx", None, None, None, None), P("wl", None, None)),
        check_vma=False,
    )
```

profile of v0, /device:TPU:12, one launch (start us, length us, event | category | flops | bytes accessed | tf_op | source)
XLA Modules:
  0.0 720.5 jit_solution(16520153187485234129)
XLA Ops:
  2.5 9.8 %copy.272 = bf16[192,8,2,1536]{3,1,2,0:T(8,128)(2,1)} copy(bf16[192,8,2,1536]{3,2,1,0:T(2,128)(2,1)} %bitcast.751) | data formatting | bytes 18874368
  12.3 12.7 %copy.114 = bf16[3072,1536]{1,0:T(8,128)(2,1)} copy(bf16[3072,1536]{0,1:T(8,128)(2,1)} %bitcast.726) | data formatting | bytes 18874368 | tf_op jit(solution)/shard_map/dot_general | solution.py:84
  27.2 6.8 fusion.29
  38.8 3.4 collective-permute-start.2
  42.2 2.5 collective-permute-start.1
  46.6 3.5 collective-permute-start.6
  51.9 4.8 collective-permute-start.5
  56.8 3.0 collective-permute-start.4
  62.3 3.5 collective-permute-start.3
  71.3 4.8 collective-permute-start.9
  88.5 3.5 collective-permute-start.10
  98.2 3.2 collective-permute-start.11
  103.3 5.9 collective-permute-done.11
  114.7 69.6 %psum.35 = f32[2,64,32]{1,2,0:T(8,128)S(1)} all-reduce(f32[2,64,32]{1,2,0:T(8,128)S(1)} %pad_maximum_fusion.1), channel_id=1, replica_groups=mesh['sy'=4,'sx'=4,'wl'=2] {'sy','sx'}, use_global_device_ids=true, to_apply=%region_0.0 | all-reduce | flops 4096 | bytes 32768 | tf_op jit(solution)/shard_map/psum | solution.py:168
  189.3 6.8 fusion.40
  199.6 72.9 %psum.36 = f32[2,64,32]{1,2,0:T(8,128)S(1)} all-reduce(f32[2,64,32]{1,2,0:T(8,128)S(1)} %pad_maximum_fusion.2), channel_id=1, replica_groups=mesh['sy'=4,'sx'=4,'wl'=2] {'sy','sx'}, use_global_device_ids=true, to_apply=%region_1.0 | all-reduce | flops 4096 | bytes 32768 | tf_op jit(solution)/shard_map/psum | solution.py:168
  274.9 3.9 collective-permute-start.13
  280.9 5.8 collective-permute-start.19
  290.5 4.8 collective-permute-start.17
  295.4 3.9 collective-permute-start.16
  302.9 3.5 collective-permute-done.15
  315.2 6.8 fusion.38
  325.4 68.3 %psum.37 = f32[2,64,32]{1,2,0:T(8,128)S(1)} all-reduce(f32[2,64,32]{1,2,0:T(8,128)S(1)} %pad_maximum_fusion.3), channel_id=1, replica_groups=mesh['sy'=4,'sx'=4,'wl'=2] {'sy','sx'}, use_global_device_ids=true, to_apply=%region_2.0 | all-reduce | flops 4096 | bytes 32768 | tf_op jit(solution)/shard_map/psum | solution.py:168
  396.2 3.9 collective-permute-start.21
  402.1 7.8 %collective-permute-start.27 = (f32[2,64,384]{2,1,0:T(8,128)}, f32[2,64,384]{2,1,0:T(8,128)S(1)}, u32[]{:S(2)}, u32[]{:S(2)}) collective-permute-start(f32[2,64,384]{2,1,0:T(8,128)} %get-tuple-element.733), channel_id=1, source_target_pairs={{2,0},{4,2},{6,4},{3,1},{5,3},{7,5},{10,8},{12,10},{14,12},{11,9},... | collective-permute-start | bytes 589832 | tf_op jit(solution)/shard_map/ppermute | solution.py:15
  413.8 4.8 collective-permute-start.25
  418.6 3.9 collective-permute-start.24
  426.2 3.5 collective-permute-done.23
  438.6 6.8 fusion.36
  448.9 68.3 %psum.38 = f32[2,64,32]{1,2,0:T(8,128)S(1)} all-reduce(f32[2,64,32]{1,2,0:T(8,128)S(1)} %pad_maximum_fusion.4), channel_id=1, replica_groups=mesh['sy'=4,'sx'=4,'wl'=2] {'sy','sx'}, use_global_device_ids=true, to_apply=%region_3.0 | all-reduce | flops 4096 | bytes 32768 | tf_op jit(solution)/shard_map/psum | solution.py:168
  519.6 3.9 collective-permute-start.29
  525.5 7.8 %collective-permute-start.35 = (f32[2,64,384]{2,1,0:T(8,128)}, f32[2,64,384]{2,1,0:T(8,128)S(1)}, u32[]{:S(2)}, u32[]{:S(2)}) collective-permute-start(f32[2,64,384]{2,1,0:T(8,128)} %get-tuple-element.729), channel_id=1, source_target_pairs={{2,0},{4,2},{6,4},{3,1},{5,3},{7,5},{10,8},{12,10},{14,12},{11,9},... | collective-permute-start | bytes 589832 | tf_op jit(solution)/shard_map/ppermute | solution.py:15
  537.2 4.8 collective-permute-start.33
  542.1 3.9 collective-permute-start.32
  549.6 3.5 collective-permute-done.31
  561.8 6.8 fusion.34
  572.0 68.5 %psum.39 = f32[2,64,32]{1,2,0:T(8,128)S(1)} all-reduce(f32[2,64,32]{1,2,0:T(8,128)S(1)} %pad_maximum_fusion.5), channel_id=1, replica_groups=mesh['sy'=4,'sx'=4,'wl'=2] {'sy','sx'}, use_global_device_ids=true, to_apply=%region_4.0 | all-reduce | flops 4096 | bytes 32768 | tf_op jit(solution)/shard_map/psum | solution.py:168
  642.9 3.9 collective-permute-start.37
  648.9 7.8 %collective-permute-start.43 = (f32[2,64,384]{2,1,0:T(8,128)S(1)}, f32[2,64,384]{2,1,0:T(8,128)S(1)}, u32[]{:S(2)}, u32[]{:S(2)}) collective-permute-start(f32[2,64,384]{2,1,0:T(8,128)S(1)} %get-tuple-element.725), channel_id=1, source_target_pairs={{2,0},{4,2},{6,4},{3,1},{5,3},{7,5},{10,8},{12,10},{14,12},{11,9},... | collective-permute-start | bytes 589832 | tf_op jit(solution)/shard_map/ppermute | solution.py:15
  660.5 4.8 collective-permute-start.41
  665.4 3.9 collective-permute-start.40
  672.9 3.5 collective-permute-done.39
  679.7 6.8 fusion.32
  689.3 3.9 collective-permute-start.45
  699.9 3.0 collective-permute-start.44
  702.9 3.9 collective-permute-start.50
  706.8 3.7 collective-permute-start.49
  710.6 3.9 collective-permute-start.47
  (406 shorter events, 155.8 us)
Async XLA Ops:
  36.2 43.0 %collective-permute-start.7 = (f32[2,64,384]{2,1,0:T(8,128)}, f32[2,64,384]{2,1,0:T(8,128)S(1)}, u32[]{:S(2)}, u32[]{:S(2)}) collective-permute-start(f32[2,64,384]{2,1,0:T(8,128)} %get-tuple-element.741), channel_id=1, source_target_pairs={{2,0},{4,2},{6,4},{3,1},{5,3},{7,5},{10,8},{12,10},{14,12},{11,9},... | collective-permute-start | bytes 589832 | tf_op jit(solution)/shard_map/ppermute | solution.py:15
  38.8 13.1 %collective-permute-start.2 = (f32[1,2,2,64]{3,2,1,0:T(2,128)S(1)}, f32[1,2,2,64]{3,2,1,0:T(2,128)S(1)}, u32[]{:S(2)}, u32[]{:S(2)}) collective-permute-start(f32[1,2,2,64]{3,2,1,0:T(2,128)S(1)} %maximum_bitcast_fusion.7), channel_id=1, source_target_pairs={{8,0},{16,8},{24,16},{9,1},{17,9},{25,17},{10,2},{18,10},{26,18},{... | collective-permute-start | bytes 3080 | tf_op jit(solution)/shard_map/ppermute | solution.py:26
  42.2 14.5 %collective-permute-start.1 = (f32[1,2,2,64]{3,2,1,0:T(2,128)S(1)}, f32[1,2,2,64]{3,2,1,0:T(2,128)S(1)}, u32[]{:S(2)}, u32[]{:S(2)}) collective-permute-start(f32[1,2,2,64]{3,2,1,0:T(2,128)S(1)} %maximum_bitcast_fusion.6), channel_id=1, source_target_pairs={{0,8},{8,16},{16,24},{1,9},{9,17},{17,25},{2,10},{10,18},{18,26},{... | collective-permute-start | bytes 3080 | tf_op jit(solution)/shard_map/ppermute | solution.py:25
  44.7 26.6 %collective-permute-start = (f32[2,64,384]{2,1,0:T(8,128)S(1)}, f32[2,64,384]{2,1,0:T(8,128)}, u32[]{:S(2)}, u32[]{:S(2)}) collective-permute-start(f32[2,64,384]{2,1,0:T(8,128)S(1)} %get-tuple-element.740), channel_id=1, source_target_pairs={{0,8},{8,16},{16,24},{1,9},{9,17},{17,25},{2,10},{10,18},{18,26},{... | collective-permute-start | bytes 589832 | tf_op jit(solution)/shard_map/ppermute | solution.py:15
  46.6 29.5 %collective-permute-start.6 = (f32[2,64,384]{2,1,0:T(8,128)}, f32[2,64,384]{2,1,0:T(8,128)}, u32[]{:S(2)}, u32[]{:S(2)}) collective-permute-start(f32[2,64,384]{2,1,0:T(8,128)} %get-tuple-element.743), channel_id=1, source_target_pairs={{0,2},{2,4},{4,6},{1,3},{3,5},{5,7},{8,10},{10,12},{12,14},{9,11},... | collective-permute-start | bytes 589832 | tf_op jit(solution)/shard_map/ppermute | solution.py:15
  51.9 31.4 %collective-permute-start.5 = (f32[2,64,384]{2,1,0:T(8,128)}, f32[2,64,384]{2,1,0:T(8,128)}, u32[]{:S(2)}, u32[]{:S(2)}) collective-permute-start(f32[2,64,384]{2,1,0:T(8,128)} %get-tuple-element.742), channel_id=1, source_target_pairs={{8,0},{16,8},{24,16},{9,1},{17,9},{25,17},{10,2},{18,10},{26,18},{... | collective-permute-start | bytes 589832 | tf_op jit(solution)/shard_map/ppermute | solution.py:15
  56.8 5.5 collective-permute-start.4
  62.3 5.5 collective-permute-start.3
  67.8 18.6 %collective-permute-start.8 = (f32[1,3,2,32,384]{4,3,2,1,0:T(8,128)}, f32[1,3,2,32,384]{4,3,2,1,0:T(8,128)S(1)}, u32[]{:S(2)}, u32[]{:S(2)}) collective-permute-start(f32[1,3,2,32,384]{4,3,2,1,0:T(8,128)} %maximum_bitcast_fusion.3), channel_id=1, source_target_pairs={{0,8},{8,16},{16,24},{1,9},{9,17},{17,25},{2,10},{10,18},{18,26},{... | collective-permute-start | bytes 884744 | tf_op jit(solution)/shard_map/ppermute | solution.py:25
  71.3 16.2 %collective-permute-start.9 = (f32[1,3,2,32,384]{4,3,2,1,0:T(8,128)}, f32[1,3,2,32,384]{4,3,2,1,0:T(8,128)S(1)}, u32[]{:S(2)}, u32[]{:S(2)}) collective-permute-start(f32[1,3,2,32,384]{4,3,2,1,0:T(8,128)} %maximum_bitcast_fusion.4), channel_id=1, source_target_pairs={{8,0},{16,8},{24,16},{9,1},{17,9},{25,17},{10,2},{18,10},{26,18},{... | collective-permute-start | bytes 884744 | tf_op jit(solution)/shard_map/ppermute | solution.py:26
  88.5 12.9 %collective-permute-start.10 = (f32[5,1,2,32,384]{4,3,2,1,0:T(8,128)}, f32[5,1,2,32,384]{4,3,2,1,0:T(8,128)}, u32[]{:S(2)}, u32[]{:S(2)}) collective-permute-start(f32[5,1,2,32,384]{4,3,2,1,0:T(8,128)} %get-tuple-element.718), channel_id=1, source_target_pairs={{0,2},{2,4},{4,6},{1,3},{3,5},{5,7},{8,10},{10,12},{12,14},{9,11},... | collective-permute-start | bytes 1474568 | tf_op jit(solution)/shard_map/ppermute | solution.py:25
  98.2 11.0 %collective-permute-start.11 = (f32[5,1,2,32,384]{4,3,2,1,0:T(8,128)}, f32[5,1,2,32,384]{4,3,2,1,0:T(8,128)}, u32[]{:S(2)}, u32[]{:S(2)}) collective-permute-start(f32[5,1,2,32,384]{4,3,2,1,0:T(8,128)} %get-tuple-element.719), channel_id=1, source_target_pairs={{2,0},{4,2},{6,4},{3,1},{5,3},{7,5},{10,8},{12,10},{14,12},{11,9},... | collective-permute-start | bytes 1474568 | tf_op jit(solution)/shard_map/ppermute | solution.py:26
  273.0 17.5 %collective-permute-start.14 = (f32[1,2,2,64]{3,2,1,0:T(2,128)S(1)}, f32[1,2,2,64]{3,2,1,0:T(2,128)S(1)}, u32[]{:S(2)}, u32[]{:S(2)}) collective-permute-start(f32[1,2,2,64]{3,2,1,0:T(2,128)S(1)} %maximum_bitcast_fusion.9), channel_id=1, source_target_pairs={{8,0},{16,8},{24,16},{9,1},{17,9},{25,17},{10,2},{18,10},{26,18},{... | collective-permute-start | bytes 3080 | tf_op jit(solution)/shard_map/ppermute | solution.py:26
  274.9 20.4 %collective-permute-start.13 = (f32[1,2,2,64]{3,2,1,0:T(2,128)S(1)}, f32[1,2,2,64]{3,2,1,0:T(2,128)S(1)}, u32[]{:S(2)}, u32[]{:S(2)}) collective-permute-start(f32[1,2,2,64]{3,2,1,0:T(2,128)S(1)} %maximum_bitcast_fusion.8), channel_id=1, source_target_pairs={{0,8},{8,16},{16,24},{1,9},{9,17},{17,25},{2,10},{10,18},{18,26},{... | collective-permute-start | bytes 3080 | tf_op jit(solution)/shard_map/ppermute | solution.py:25
  280.9 28.2 %collective-permute-start.19 = (f32[2,64,384]{2,1,0:T(8,128)}, f32[2,64,384]{2,1,0:T(8,128)S(1)}, u32[]{:S(2)}, u32[]{:S(2)}) collective-permute-start(f32[2,64,384]{2,1,0:T(8,128)} %get-tuple-element.737), channel_id=1, source_target_pairs={{2,0},{4,2},{6,4},{3,1},{5,3},{7,5},{10,8},{12,10},{14,12},{11,9},... | collective-permute-start | bytes 589832 | tf_op jit(solution)/shard_map/ppermute | solution.py:15
  286.6 20.1 %collective-permute-start.12 = (f32[2,64,384]{2,1,0:T(8,128)}, f32[2,64,384]{2,1,0:T(8,128)}, u32[]{:S(2)}, u32[]{:S(2)}) collective-permute-start(f32[2,64,384]{2,1,0:T(8,128)} %get-tuple-element.736), channel_id=1, source_target_pairs={{0,8},{8,16},{16,24},{1,9},{9,17},{17,25},{2,10},{10,18},{18,26},{... | collective-permute-start | bytes 589832 | tf_op jit(solution)/shard_map/ppermute | solution.py:15
  288.6 18.1 %collective-permute-start.18 = (f32[2,64,384]{2,1,0:T(8,128)}, f32[2,64,384]{2,1,0:T(8,128)S(1)}, u32[]{:S(2)}, u32[]{:S(2)}) collective-permute-start(f32[2,64,384]{2,1,0:T(8,128)} %get-tuple-element.739), channel_id=1, source_target_pairs={{0,2},{2,4},{4,6},{1,3},{3,5},{5,7},{8,10},{10,12},{12,14},{9,11},... | collective-permute-start | bytes 589832 | tf_op jit(solution)/shard_map/ppermute | solution.py:15
  290.5 19.9 %collective-permute-start.17 = (f32[2,64,384]{2,1,0:T(8,128)}, f32[2,64,384]{2,1,0:T(8,128)S(1)}, u32[]{:S(2)}, u32[]{:S(2)}) collective-permute-start(f32[2,64,384]{2,1,0:T(8,128)} %get-tuple-element.738), channel_id=1, source_target_pairs={{8,0},{16,8},{24,16},{9,1},{17,9},{25,17},{10,2},{18,10},{26,18},{... | collective-permute-start | bytes 589832 | tf_op jit(solution)/shard_map/ppermute | solution.py:15
  295.4 5.5 collective-permute-start.16
  394.2 19.5 %collective-permute-start.22 = (f32[1,2,2,64]{3,2,1,0:T(2,128)S(1)}, f32[1,2,2,64]{3,2,1,0:T(2,128)S(1)}, u32[]{:S(2)}, u32[]{:S(2)}) collective-permute-start(f32[1,2,2,64]{3,2,1,0:T(2,128)S(1)} %maximum_bitcast_fusion.11), channel_id=1, source_target_pairs={{8,0},{16,8},{24,16},{9,1},{17,9},{25,17},{10,2},{18,10},{26,18},{... | collective-permute-start | bytes 3080 | tf_op jit(solution)/shard_map/ppermute | solution.py:26
  396.2 22.4 %collective-permute-start.21 = (f32[1,2,2,64]{3,2,1,0:T(2,128)S(1)}, f32[1,2,2,64]{3,2,1,0:T(2,128)S(1)}, u32[]{:S(2)}, u32[]{:S(2)}) collective-permute-start(f32[1,2,2,64]{3,2,1,0:T(2,128)S(1)} %maximum_bitcast_fusion.10), channel_id=1, source_target_pairs={{0,8},{8,16},{16,24},{1,9},{9,17},{17,25},{2,10},{10,18},{18,26},{... | collective-permute-start | bytes 3080 | tf_op jit(solution)/shard_map/ppermute | solution.py:25
  402.1 30.3 %collective-permute-start.27 = (f32[2,64,384]{2,1,0:T(8,128)}, f32[2,64,384]{2,1,0:T(8,128)S(1)}, u32[]{:S(2)}, u32[]{:S(2)}) collective-permute-start(f32[2,64,384]{2,1,0:T(8,128)} %get-tuple-element.733), channel_id=1, source_target_pairs={{2,0},{4,2},{6,4},{3,1},{5,3},{7,5},{10,8},{12,10},{14,12},{11,9},... | collective-permute-start | bytes 589832 | tf_op jit(solution)/shard_map/ppermute | solution.py:15
  409.9 20.1 %collective-permute-start.20 = (f32[2,64,384]{2,1,0:T(8,128)}, f32[2,64,384]{2,1,0:T(8,128)}, u32[]{:S(2)}, u32[]{:S(2)}) collective-permute-start(f32[2,64,384]{2,1,0:T(8,128)} %get-tuple-element.732), channel_id=1, source_target_pairs={{0,8},{8,16},{16,24},{1,9},{9,17},{17,25},{2,10},{10,18},{18,26},{... | collective-permute-start | bytes 589832 | tf_op jit(solution)/shard_map/ppermute | solution.py:15
  411.8 18.1 %collective-permute-start.26 = (f32[2,64,384]{2,1,0:T(8,128)}, f32[2,64,384]{2,1,0:T(8,128)S(1)}, u32[]{:S(2)}, u32[]{:S(2)}) collective-permute-start(f32[2,64,384]{2,1,0:T(8,128)} %get-tuple-element.735), channel_id=1, source_target_pairs={{0,2},{2,4},{4,6},{1,3},{3,5},{5,7},{8,10},{10,12},{12,14},{9,11},... | collective-permute-start | bytes 589832 | tf_op jit(solution)/shard_map/ppermute | solution.py:15
  413.8 19.9 %collective-permute-start.25 = (f32[2,64,384]{2,1,0:T(8,128)}, f32[2,64,384]{2,1,0:T(8,128)S(1)}, u32[]{:S(2)}, u32[]{:S(2)}) collective-permute-start(f32[2,64,384]{2,1,0:T(8,128)} %get-tuple-element.734), channel_id=1, source_target_pairs={{8,0},{16,8},{24,16},{9,1},{17,9},{25,17},{10,2},{18,10},{26,18},{... | collective-permute-start | bytes 589832 | tf_op jit(solution)/shard_map/ppermute | solution.py:15
  418.6 5.5 collective-permute-start.24
  517.7 19.5 %collective-permute-start.30 = (f32[1,2,2,64]{3,2,1,0:T(2,128)S(1)}, f32[1,2,2,64]{3,2,1,0:T(2,128)S(1)}, u32[]{:S(2)}, u32[]{:S(2)}) collective-permute-start(f32[1,2,2,64]{3,2,1,0:T(2,128)S(1)} %maximum_bitcast_fusion.13), channel_id=1, source_target_pairs={{8,0},{16,8},{24,16},{9,1},{17,9},{25,17},{10,2},{18,10},{26,18},{... | collective-permute-start | bytes 3080 | tf_op jit(solution)/shard_map/ppermute | solution.py:26
  519.6 22.4 %collective-permute-start.29 = (f32[1,2,2,64]{3,2,1,0:T(2,128)S(1)}, f32[1,2,2,64]{3,2,1,0:T(2,128)S(1)}, u32[]{:S(2)}, u32[]{:S(2)}) collective-permute-start(f32[1,2,2,64]{3,2,1,0:T(2,128)S(1)} %maximum_bitcast_fusion.12), channel_id=1, source_target_pairs={{0,8},{8,16},{16,24},{1,9},{9,17},{17,25},{2,10},{10,18},{18,26},{... | collective-permute-start | bytes 3080 | tf_op jit(solution)/shard_map/ppermute | solution.py:25
  525.5 30.3 %collective-permute-start.35 = (f32[2,64,384]{2,1,0:T(8,128)}, f32[2,64,384]{2,1,0:T(8,128)S(1)}, u32[]{:S(2)}, u32[]{:S(2)}) collective-permute-start(f32[2,64,384]{2,1,0:T(8,128)} %get-tuple-element.729), channel_id=1, source_target_pairs={{2,0},{4,2},{6,4},{3,1},{5,3},{7,5},{10,8},{12,10},{14,12},{11,9},... | collective-permute-start | bytes 589832 | tf_op jit(solution)/shard_map/ppermute | solution.py:15
  533.3 20.1 %collective-permute-start.28 = (f32[2,64,384]{2,1,0:T(8,128)}, f32[2,64,384]{2,1,0:T(8,128)}, u32[]{:S(2)}, u32[]{:S(2)}) collective-permute-start(f32[2,64,384]{2,1,0:T(8,128)} %get-tuple-element.728), channel_id=1, source_target_pairs={{0,8},{8,16},{16,24},{1,9},{9,17},{17,25},{2,10},{10,18},{18,26},{... | collective-permute-start | bytes 589832 | tf_op jit(solution)/shard_map/ppermute | solution.py:15
  535.3 18.1 %collective-permute-start.34 = (f32[2,64,384]{2,1,0:T(8,128)}, f32[2,64,384]{2,1,0:T(8,128)S(1)}, u32[]{:S(2)}, u32[]{:S(2)}) collective-permute-start(f32[2,64,384]{2,1,0:T(8,128)} %get-tuple-element.731), channel_id=1, source_target_pairs={{0,2},{2,4},{4,6},{1,3},{3,5},{5,7},{8,10},{10,12},{12,14},{9,11},... | collective-permute-start | bytes 589832 | tf_op jit(solution)/shard_map/ppermute | solution.py:15
  537.2 19.9 %collective-permute-start.33 = (f32[2,64,384]{2,1,0:T(8,128)}, f32[2,64,384]{2,1,0:T(8,128)S(1)}, u32[]{:S(2)}, u32[]{:S(2)}) collective-permute-start(f32[2,64,384]{2,1,0:T(8,128)} %get-tuple-element.730), channel_id=1, source_target_pairs={{8,0},{16,8},{24,16},{9,1},{17,9},{25,17},{10,2},{18,10},{26,18},{... | collective-permute-start | bytes 589832 | tf_op jit(solution)/shard_map/ppermute | solution.py:15
  542.1 5.5 collective-permute-start.32
  641.0 19.5 %collective-permute-start.38 = (f32[1,2,2,64]{3,2,1,0:T(2,128)S(1)}, f32[1,2,2,64]{3,2,1,0:T(2,128)S(1)}, u32[]{:S(2)}, u32[]{:S(2)}) collective-permute-start(f32[1,2,2,64]{3,2,1,0:T(2,128)S(1)} %maximum_bitcast_fusion.15), channel_id=1, source_target_pairs={{8,0},{16,8},{24,16},{9,1},{17,9},{25,17},{10,2},{18,10},{26,18},{... | collective-permute-start | bytes 3080 | tf_op jit(solution)/shard_map/ppermute | solution.py:26
  642.9 22.4 %collective-permute-start.37 = (f32[1,2,2,64]{3,2,1,0:T(2,128)S(1)}, f32[1,2,2,64]{3,2,1,0:T(2,128)S(1)}, u32[]{:S(2)}, u32[]{:S(2)}) collective-permute-start(f32[1,2,2,64]{3,2,1,0:T(2,128)S(1)} %maximum_bitcast_fusion.14), channel_id=1, source_target_pairs={{0,8},{8,16},{16,24},{1,9},{9,17},{17,25},{2,10},{10,18},{18,26},{... | collective-permute-start | bytes 3080 | tf_op jit(solution)/shard_map/ppermute | solution.py:25
  648.9 28.1 %collective-permute-start.43 = (f32[2,64,384]{2,1,0:T(8,128)S(1)}, f32[2,64,384]{2,1,0:T(8,128)S(1)}, u32[]{:S(2)}, u32[]{:S(2)}) collective-permute-start(f32[2,64,384]{2,1,0:T(8,128)S(1)} %get-tuple-element.725), channel_id=1, source_target_pairs={{2,0},{4,2},{6,4},{3,1},{5,3},{7,5},{10,8},{12,10},{14,12},{11,9},... | collective-permute-start | bytes 589832 | tf_op jit(solution)/shard_map/ppermute | solution.py:15
  656.7 20.1 %collective-permute-start.36 = (f32[2,64,384]{2,1,0:T(8,128)}, f32[2,64,384]{2,1,0:T(8,128)S(1)}, u32[]{:S(2)}, u32[]{:S(2)}) collective-permute-start(f32[2,64,384]{2,1,0:T(8,128)} %get-tuple-element.724), channel_id=1, source_target_pairs={{0,8},{8,16},{16,24},{1,9},{9,17},{17,25},{2,10},{10,18},{18,26},{... | collective-permute-start | bytes 589832 | tf_op jit(solution)/shard_map/ppermute | solution.py:15
  658.6 18.2 %collective-permute-start.42 = (f32[2,64,384]{2,1,0:T(8,128)}, f32[2,64,384]{2,1,0:T(8,128)S(1)}, u32[]{:S(2)}, u32[]{:S(2)}) collective-permute-start(f32[2,64,384]{2,1,0:T(8,128)} %get-tuple-element.727), channel_id=1, source_target_pairs={{0,2},{2,4},{4,6},{1,3},{3,5},{5,7},{8,10},{10,12},{12,14},{9,11},... | collective-permute-start | bytes 589832 | tf_op jit(solution)/shard_map/ppermute | solution.py:15
  660.5 16.9 %collective-permute-start.41 = (f32[2,64,384]{2,1,0:T(8,128)S(1)}, f32[2,64,384]{2,1,0:T(8,128)S(1)}, u32[]{:S(2)}, u32[]{:S(2)}) collective-permute-start(f32[2,64,384]{2,1,0:T(8,128)S(1)} %get-tuple-element.726), channel_id=1, source_target_pairs={{8,0},{16,8},{24,16},{9,1},{17,9},{25,17},{10,2},{18,10},{26,18},{... | collective-permute-start | bytes 589832 | tf_op jit(solution)/shard_map/ppermute | solution.py:15
  665.4 5.5 collective-permute-start.40
  687.4 6.5 collective-permute-start.46
  689.3 6.4 collective-permute-start.45
  695.7 14.8 %collective-permute-start.48 = (f32[4,1,2,64]{3,2,1,0:T(2,128)S(1)}, f32[4,1,2,64]{3,2,1,0:T(2,128)S(1)}, u32[]{:S(2)}, u32[]{:S(2)}) collective-permute-start(f32[4,1,2,64]{3,2,1,0:T(2,128)S(1)} %get-tuple-element.813), channel_id=1, source_target_pairs={{2,0},{4,2},{6,4},{3,1},{5,3},{7,5},{10,8},{12,10},{14,12},{11,9},... | collective-permute-start | bytes 6152 | tf_op jit(solution)/shard_map/ppermute | solution.py:26
  697.9 18.7 %collective-permute-start.51 = (f32[2,64,384]{2,1,0:T(8,128)S(1)}, f32[2,64,384]{2,1,0:T(8,128)S(1)}, u32[]{:S(2)}, u32[]{:S(2)}) collective-permute-start(f32[2,64,384]{2,1,0:T(8,128)S(1)} %get-tuple-element.722), channel_id=1, source_target_pairs={{2,0},{4,2},{6,4},{3,1},{5,3},{7,5},{10,8},{12,10},{14,12},{11,9},... | collective-permute-start | bytes 589832 | tf_op jit(solution)/shard_map/ppermute | solution.py:15
  699.9 16.5 %collective-permute-start.44 = (f32[2,64,384]{2,1,0:T(8,128)S(1)}, f32[2,64,384]{2,1,0:T(8,128)S(1)}, u32[]{:S(2)}, u32[]{:S(2)}) collective-permute-start(f32[2,64,384]{2,1,0:T(8,128)S(1)} %get-tuple-element.720), channel_id=1, source_target_pairs={{0,8},{8,16},{16,24},{1,9},{9,17},{17,25},{2,10},{10,18},{18,26},{... | collective-permute-start | bytes 589832 | tf_op jit(solution)/shard_map/ppermute | solution.py:15
  702.9 13.5 %collective-permute-start.50 = (f32[2,64,384]{2,1,0:T(8,128)S(1)}, f32[2,64,384]{2,1,0:T(8,128)S(1)}, u32[]{:S(2)}, u32[]{:S(2)}) collective-permute-start(f32[2,64,384]{2,1,0:T(8,128)S(1)} %get-tuple-element.723), channel_id=1, source_target_pairs={{0,2},{2,4},{4,6},{1,3},{3,5},{5,7},{8,10},{10,12},{12,14},{9,11},... | collective-permute-start | bytes 589832 | tf_op jit(solution)/shard_map/ppermute | solution.py:15
  706.8 10.3 %collective-permute-start.49 = (f32[2,64,384]{2,1,0:T(8,128)S(1)}, f32[2,64,384]{2,1,0:T(8,128)S(1)}, u32[]{:S(2)}, u32[]{:S(2)}) collective-permute-start(f32[2,64,384]{2,1,0:T(8,128)S(1)} %get-tuple-element.721), channel_id=1, source_target_pairs={{8,0},{16,8},{24,16},{9,1},{17,9},{25,17},{10,2},{18,10},{26,18},{... | collective-permute-start | bytes 589832 | tf_op jit(solution)/shard_map/ppermute | solution.py:15
  710.6 5.5 collective-permute-start.47
  (10 other events, 137.0 us)
where the time goes:
time: 732 us; the launch traced here: 720 us
  blocking collectives  348 us (48%)
  starting transfers between devices  173 us (24%)
  local copies, waits for them, and re-layouts  74.8 us (10%)
  matrix products  67.9 us (9%)
  waiting for transfers between devices  28.6 us (4%)
  other arithmetic  24.6 us (3%)
    psum x5, blocking collectives, per_device(): lax.psum(restrict_sum(outgoing, sender_weights), ('sy', 'sx'))  348 us
    ppermute x24, starting transfers between devices, shifted(): return lax.ppermute(value, axis, pairs)  88.9 us
    ppermute x14, starting transfers between devices, with_halo(): before = lax.ppermute(last, axis, up)  42.4 us
    ppermute x14, starting transfers between devices, with_halo(): after = lax.ppermute(initial, axis, down)  41.8 us
    dot_general x6, matrix products, outgoing_traces(): jnp.dot(row_block, map_table, preferred_element_type=jnp.float32)  40.6 us
    ppermute x14, waiting for transfers between devices, with_halo(): before = lax.ppermute(last, axis, up)  18.4 us
  transfers between devices with their start and end apart: 52, of which 13 were waited for; matrix products, arithmetic and copies ran while one was open for 7% of the time, Pallas kernels for 0%

commit v1 on v0

v1 whole, which is shorter than its diff:
```python
import functools

import jax
import jax.numpy as jnp
from jax import lax
from jax.experimental import pallas as pl
from jax.experimental.pallas import tpu as pltpu
from jax.sharding import PartitionSpec as P

ITERS = 6
LANES = 128
F32, BF16 = jnp.float32, jnp.bfloat16
MESH = pl.DeviceIdType.MESH
PRECISE = lax.Precision.HIGHEST
NT = (((1,), (1,)), ((), ()))


def dot(a, b):
    return jnp.dot(a, b, preferred_element_type=F32)


def dot_nt(a, b):
    return lax.dot_general(a, b, NT, preferred_element_type=F32)


def split(x):
    hi = x.astype(BF16)
    return hi, (x - hi.astype(F32)).astype(BF16)


def sweep_kernel(
    ny, nx, iters,
    map_ref, src_ref, rest_ref, lift_ref, inv_ref,
    traces_ref, coef_ref,
    out, recv, wrecv, cbuf, crecv, wcbuf, wcrecv, lhs, ext_lhs, ext_rhs,
    wts, part, xs, rowsum, ys,
    side_send, side_recv, diag_send, diag_recv,
    wside_send, wside_recv, wdiag_send, wdiag_recv,
    x_send, x_recv, y_send, y_recv,
):
    rows, k = src_ref.shape
    side = k // 4
    nsrc = rows // 2
    nw_rows = rest_ref.shape[0]
    nc = nw_rows // 2
    half = nsrc // 2
    y, x = lax.axis_index("sy"), lax.axis_index("sx")
    up, dn, lf, rt = y > 0, y < ny - 1, x > 0, x < nx - 1
    sides = ((up, -1, 0), (dn, 1, 0), (lf, 0, -1), (rt, 0, 1))
    diags = (
        (up & lf, -1, -1),
        (up & rt, -1, 1),
        (dn & lf, 1, -1),
        (dn & rt, 1, 1),
    )

    def lanes(s):
        return pl.ds(s * side, side)

    def copies(src, dst, corner_src, corner_dst, ssem, rsem, dsem, drsem):
        flat, diag, flat_in, diag_in = [], [], [], []
        for d, (cond, dy, dx) in enumerate(sides):
            o = d ^ 1
            dev = {"sy": y + dy, "sx": x + dx}
            flat.append((cond, pltpu.make_async_remote_copy(
                src.at[:, lanes(d)], dst.at[:, lanes(o)], ssem.at[d], rsem.at[o],
                device_id=dev, device_id_type=MESH)))
            flat_in.append((cond, pltpu.make_async_remote_copy(
                src.at[:, lanes(d)], dst.at[:, lanes(d)], ssem.at[d], rsem.at[d],
                device_id=dev, device_id_type=MESH)))
        for d, (cond, dy, dx) in enumerate(diags):
            o = 3 - d
            dev = {"sy": y + dy, "sx": x + dx}
            diag.append((cond, pltpu.make_async_remote_copy(
                corner_src, corner_dst.at[o], dsem.at[d], drsem.at[o],
                device_id=dev, device_id_type=MESH)))
            diag_in.append((cond, pltpu.make_async_remote_copy(
                corner_src, corner_dst.at[d], dsem.at[d], drsem.at[d],
                device_id=dev, device_id_type=MESH)))
        return flat, diag, flat_in, diag_in

    def each(items, what):
        for cond, c in items:
            pl.when(cond)(getattr(c, what))

    def pack_corners(ref, dst, scale):
        def column(s, last):
            if last:
                return ref[:, (s + 1) * side - LANES:(s + 1) * side][:, LANES - 1:]
            return ref[:, s * side:s * side + LANES][:, 0:1]

        n = ref.shape[0]
        lane = lax.broadcasted_iota(jnp.int32, (n, LANES), 1)
        block = jnp.zeros((n, LANES), F32)
        for j, (a, b) in enumerate((
            ((0, 0), (2, 0)), ((0, 1), (3, 0)), ((1, 0), (2, 1)), ((1, 1), (3, 1)),
        )):
            block = jnp.where(lane == j, column(*a) + column(*b), block)
        if scale != 1.0:
            block = block * scale
        if n < LANES:
            block = jnp.concatenate([block, jnp.zeros((LANES - n, LANES), F32)], axis=0)
        dst[...] = block.T[:8]

    def assemble(get, get_corner, n, scale, write):
        row = lax.broadcasted_iota(jnp.int32, (LANES, LANES), 0)
        block = jnp.zeros((LANES, LANES), F32)
        for j in range(4):
            block = jnp.where(row == j, get_corner(j)[3 - j:4 - j], block)
        cols = block.T[:n] * scale
        lane = lax.broadcasted_iota(jnp.int32, (n, LANES), 1)
        ends = ((0, 1), (2, 3), (0, 2), (1, 3))
        for s in range(4):
            for t in range(side // LANES):
                at = s * side + t * LANES
                v = get(at)
                if t == 0:
                    j = ends[s][0]
                    v = v + jnp.where(lane == 0, cols[:, j:j + 1], 0.0)
                if t == side // LANES - 1:
                    j = ends[s][1]
                    v = v + jnp.where(lane == LANES - 1, cols[:, j:j + 1], 0.0)
                write(at, v)

    for d, (cond, _, _) in enumerate(sides):
        @pl.when(jnp.logical_not(cond))
        def _(d=d):
            for slot in range(2):
                recv[slot, :, lanes(d)] = jnp.zeros((rows, side), F32)
            wrecv[:, lanes(d)] = jnp.zeros((nw_rows, side), F32)
    for d, (cond, _, _) in enumerate(diags):
        @pl.when(jnp.logical_not(cond))
        def _(d=d):
            for slot in range(2):
                crecv[slot, d] = jnp.zeros((8, LANES), F32)
            wcrecv[d] = jnp.zeros((8, LANES), F32)

    w_flat, w_diag, w_flat_in, w_diag_in = copies(
        rest_ref, wrecv, wcbuf, wcrecv, wside_send, wside_recv, wdiag_send, wdiag_recv)
    pack_corners(rest_ref, wcbuf, 0.5)
    each(w_diag, "start")
    each(w_flat, "start")

    def exchange(slot, src):
        return copies(
            src, recv.at[slot], cbuf.at[slot], crecv.at[slot],
            side_send.at[slot], side_recv.at[slot], diag_send.at[slot], diag_recv.at[slot])

    def x_copies(slot):
        res = []
        for d in range(1, nx):
            peer = lax.rem(x + d, nx)
            res.append((
                pltpu.make_async_remote_copy(
                    part.at[slot], xs.at[slot, x], x_send.at[slot, d], x_recv.at[slot, d],
                    device_id={"sy": y, "sx": peer}, device_id_type=MESH),
                pltpu.make_async_remote_copy(
                    part.at[slot], xs.at[slot, lax.rem(x + nx - d, nx)],
                    x_send.at[slot, d], x_recv.at[slot, d],
                    device_id={"sy": y, "sx": peer}, device_id_type=MESH)))
        return res

    def y_copies(slot):
        res = []
        for d in range(1, ny):
            peer = lax.rem(y + d, ny)
            res.append((
                pltpu.make_async_remote_copy(
                    rowsum.at[slot], ys.at[slot, y], y_send.at[slot, d], y_recv.at[slot, d],
                    device_id={"sy": peer, "sx": x}, device_id_type=MESH),
                pltpu.make_async_remote_copy(
                    rowsum.at[slot], ys.at[slot, lax.rem(y + ny - d, ny)],
                    y_send.at[slot, d], y_recv.at[slot, d],
                    device_id={"sy": peer, "sx": x}, device_id_type=MESH)))
        return res

    def restrict_start(slot, src):
        re_hi, re_lo = split(src[:nsrc])
        im_hi, im_lo = split(src[nsrc:])
        a_hi, a_lo, b_hi, b_lo = (wts[i] for i in range(4))
        t = dot_nt(re_hi, a_hi) + dot_nt(im_hi, b_hi)
        t = t + (dot_nt(re_lo, a_hi) + dot_nt(im_lo, b_hi))
        t = t + (dot_nt(re_hi, a_lo) + dot_nt(im_hi, b_lo))
        lane = lax.broadcasted_iota(jnp.int32, (half, LANES), 1)
        t = jnp.where(lane < 2 * nc, t[:half], t[half:])
        part[slot] = t
        xs[slot, x] = t
        for c, _ in x_copies(slot):
            c.start()

    def restrict_turn(slot):
        for _, c in x_copies(slot):
            c.wait_recv()
        t = xs[slot, 0]
        for i in range(1, nx):
            t = t + xs[slot, i]
        rowsum[slot] = t
        ys[slot, y] = t
        for c, _ in y_copies(slot):
            c.start()

    def coarse(slot):
        for _, c in y_copies(slot):
            c.wait_recv()
        t = ys[slot, 0]
        for i in range(1, ny):
            t = t + ys[slot, i]
        lane = lax.broadcasted_iota(jnp.int32, (half, LANES), 1)
        low = lane < 2 * nc
        t = jnp.concatenate([jnp.where(low, t, 0.0), jnp.where(low, 0.0, t)], axis=0)
        c_re = jnp.dot(t, inv_ref[0], preferred_element_type=F32, precision=PRECISE)
        c_im = jnp.dot(t, inv_ref[1], preferred_element_type=F32, precision=PRECISE)
        c = jnp.concatenate([c_re, c_im], axis=0)
        coef_ref[...] = c
        hi, lo = split(c)
        lane = lax.broadcasted_iota(jnp.int32, (rows, LANES), 1)
        mid = (lane >= nc) & (lane < 2 * nc)
        ext_lhs[...] = jnp.where(mid, lo.astype(F32), hi.astype(F32)).astype(BF16)

    def restrict_end(slot):
        for c, _ in x_copies(slot):
            c.wait_send()
        for c, _ in y_copies(slot):
            c.wait_send()

    flat, diag, flat_in, diag_in = exchange(0, src_ref)
    pack_corners(src_ref, cbuf.at[0], 1.0)
    each(diag, "start")
    each(flat, "start")

    lift_hi, lift_lo = split(lift_ref[...])
    lhs[...] = jnp.concatenate([lift_hi, lift_lo], axis=0)
    for s in range(4):
        p = dot(lhs[...], map_ref[:, s * side:(s + 1) * side])
        q = dot(lhs[...], map_ref[:, k + s * side:k + (s + 1) * side])
        p = p[:nw_rows] + p[nw_rows:]
        q = q[:nw_rows] + q[nw_rows:]
        for at, v in ((s * side, p[:nc] - q[nc:]), (k + s * side, q[:nc] + p[nc:])):
            hi, lo = split(v)
            ext_rhs[:, at:at + side] = jnp.concatenate(
                [hi, hi, lo, jnp.zeros((LANES - 3 * nc, side), BF16)], axis=0)

    each(w_flat_in, "wait_recv")
    each(w_diag_in, "wait_recv")

    def write_weights(at, v):
        wr, wi = v[:nc], v[nc:]
        for i, rowset in ((0, [wr, wi, wr, wi]), (2, [-wi, wr, -wi, wr])):
            hi, lo = split(jnp.concatenate(rowset, axis=0))
            wts[i, :, at:at + LANES] = hi
            wts[i + 1, :, at:at + LANES] = lo

    assemble(lambda at: wrecv[:, at:at + LANES], lambda j: wcrecv[j], nw_rows, 1.0, write_weights)
    restrict_start(0, src_ref)
    restrict_turn(0)
    each(w_flat, "wait_send")
    each(w_diag, "wait_send")

    def store_lhs(at, v):
        lhs[:, at:at + LANES] = v.astype(BF16)

    def step(it, carry):
        old = lax.rem(it + 1, 2)
        new = lax.rem(it, 2)
        flat, diag, flat_in, diag_in = exchange(old, out)
        each(diag_in, "wait_recv")
        each(flat_in, "wait_recv")
        assemble(lambda at: recv[old, :, at:at + LANES], lambda j: crecv[old, j], rows, 0.5, store_lhs)
        each(flat, "wait_send")
        each(diag, "wait_send")
        for s in range(4):
            at = s * side
            p = dot(lhs[...], map_ref[:, at:at + side])
            q = dot(lhs[...], map_ref[:, k + at:k + at + side])
            out[:nsrc, at:at + side] = p[:nsrc] - q[nsrc:] + src_ref[:nsrc, at:at + side]
            out[nsrc:, at:at + side] = q[:nsrc] + p[nsrc:] + src_ref[nsrc:, at:at + side]
        coarse(old)
        restrict_end(old)
        for s in range(4):
            at = s * side
            p = dot(ext_lhs[...], ext_rhs[:, at:at + side])
            q = dot(ext_lhs[...], ext_rhs[:, k + at:k + at + side])
            out[:nsrc, at:at + side] += p[:nsrc] - q[nsrc:]
            out[nsrc:, at:at + side] += q[:nsrc] + p[nsrc:]
        flat, diag, _, _ = exchange(new, out)
        pack_corners(out, cbuf.at[new], 1.0)
        each(diag, "start")

        @pl.when(it < iters - 1)
        def _():
            restrict_start(new, out)

        each(flat, "start")

        @pl.when(it < iters - 1)
        def _():
            restrict_turn(new)

        return carry

    lax.fori_loop(1, iters, step, 0)

    last = (iters - 1) % 2
    flat, diag, flat_in, diag_in = exchange(last, out)
    each(diag_in, "wait_recv")
    each(flat_in, "wait_recv")

    def store_out(at, v):
        traces_ref[:, at:at + LANES] = v

    assemble(lambda at: recv[last, :, at:at + LANES], lambda j: crecv[last, j], rows, 0.5, store_out)
    each(flat, "wait_send")
    each(diag, "wait_send")


def per_device(ny, nx, interface_map, source_trace, restriction, prolongation, coarse_inverse):
    _, _, _, nsrc, _, side = source_trace.shape
    nc = restriction.shape[3]
    k, rows = 4 * side, 2 * nsrc
    table = interface_map.reshape(k, 2 * k)
    src = source_trace.reshape(rows, k)
    rest = restriction.reshape(2 * nc, k)
    lift = prolongation.reshape(2 * nc, k)
    cr, ci = coarse_inverse[0], coarse_inverse[1]

    def spread(top, bottom):
        column = jnp.concatenate([top, bottom, top, bottom], axis=0)
        blank = jnp.zeros((4 * nc, LANES - 3 * nc), F32)
        return jnp.concatenate([column, column, column, blank], axis=1)

    inv = jnp.stack([spread(cr, -ci), spread(ci, cr)])
    half = nsrc // 2
    dma = pltpu.SemaphoreType.DMA
    vmem = pl.BlockSpec(memory_space=pltpu.VMEM)
    traces, coef = pl.pallas_call(
        functools.partial(sweep_kernel, ny, nx, ITERS),
        out_shape=(
            jax.ShapeDtypeStruct((rows, k), F32),
            jax.ShapeDtypeStruct((rows, LANES), F32),
        ),
        in_specs=[vmem] * 5,
        out_specs=(vmem, vmem),
        scratch_shapes=[
            pltpu.VMEM((rows, k), F32),
            pltpu.VMEM((2, rows, k), F32),
            pltpu.VMEM((2 * nc, k), F32),
            pltpu.VMEM((2, 8, LANES), F32),
            pltpu.VMEM((2, 4, 8, LANES), F32),
            pltpu.VMEM((8, LANES), F32),
            pltpu.VMEM((4, 8, LANES), F32),
            pltpu.VMEM((rows, k), BF16),
            pltpu.VMEM((rows, LANES), BF16),
            pltpu.VMEM((LANES, 2 * k), BF16),
            pltpu.VMEM((4, 4 * nc, k), BF16),
            pltpu.VMEM((2, half, LANES), F32),
            pltpu.VMEM((2, nx, half, LANES), F32),
            pltpu.VMEM((2, half, LANES), F32),
            pltpu.VMEM((2, ny, half, LANES), F32),
            dma((2, 4)), dma((2, 4)), dma((2, 4)), dma((2, 4)),
            dma((4,)), dma((4,)), dma((4,)), dma((4,)),
            dma((2, nx)), dma((2, nx)), dma((2, ny)), dma((2, ny)),
        ],
        compiler_params=pltpu.CompilerParams(
            has_side_effects=True, vmem_limit_bytes=48 * 1024 * 1024
        ),
    )(table, src, rest, lift, inv)
    return (
        traces.reshape(source_trace.shape),
        coef.reshape(2, nsrc, LANES)[:, :, :nc],
    )


def solution(mesh):
    return jax.shard_map(
        functools.partial(per_device, mesh.shape["sy"], mesh.shape["sx"]),
        mesh=mesh,
        in_specs=(
            P(("wl", "sy"), "sx", None, None, None),
            P(("wl", "sy"), "sx", None, None, None, None),
            P(("wl", "sy"), "sx", None, None, None, None),
            P(("wl", "sy"), "sx", None, None, None, None),
            P("wl", None, None),
        ),
        out_specs=(P(("wl", "sy"), "sx", None, None, None, None), P("wl", None, None)),
        check_vma=False,
    )
```

time: 732 us -> 105 us (0.14); the launches traced: 720 us -> 104 us
  blocking collectives: 348 us -> 0 us
  starting transfers between devices: 173 us -> 0 us
  Pallas kernels: 0 us -> 86.5 us
  matrix products: 67.9 us -> 0 us
  local copies, waits for them, and re-layouts: 74.8 us -> 16 us
  waiting for transfers between devices: 28.6 us -> 0 us
  other arithmetic: 24.6 us -> 0.26 us
    psum x5 -> x0, blocking collectives: 348 us -> none  [per_device(): lax.psum(restrict_sum(outgoing, sender_weights), ('sy', 'sx'))]
    ppermute x52 -> x0, starting transfers between devices: 173 us -> none  [the longest x24 88.9 us: shifted(): return lax.ppermute(value, axis, pairs)]
    pallas_call x0 -> x1, Pallas kernels: none -> 86.5 us  [per_device(): pl.pallas_call(functools.partial(sweep_kernel, ny, nx, ITERS), out_shape=...]
    dot_general x72 -> x0, matrix products: 67.9 us -> none  [the longest x6 40.6 us: outgoing_traces(): jnp.dot(row_block, map_table, preferred_element_type=jnp.float32)]
    scatter-add x56 -> x0, local copies, waits for them, and re-layouts: 31.3 us -> none  [the longest x12 14.3 us: assemble(): from_north.at[..., 0].add(0.5 * into_northwest).at[..., -1]]
    ppermute x52 -> x0, waiting for transfers between devices: 28.6 us -> none  [the longest x14 18.4 us: with_halo(): before = lax.ppermute(last, axis, up)]
    dot_general x1 -> x0, local copies, waits for them, and re-layouts: 12.7 us -> none  [outgoing_traces(): jnp.dot(row_block, map_table, preferred_element_type=jnp.float32)]
    add x26 -> x0, other arithmetic: 9.22 us -> none  [the longest x6 4.17 us: assemble(): from_north.at[..., 0].add(0.5 * into_northwest).at[..., -1]]
  transfers between devices with their start and end apart: 52 -> 0, of which waited for: 13 -> 0; matrix products, arithmetic and copies ran while one was open for 7% -> 0% of each run, Pallas kernels for 0% -> 0%
where the time goes in v1:
time: 105 us; the launch traced here: 104 us
  Pallas kernels  86.5 us (82%)
  local copies, waits for them, and re-layouts  16 us (15%)
    pallas_call x1, Pallas kernels, per_device(): pl.pallas_call(functools.partial(sweep_kernel, ny, nx, ITERS), out_shape=...  86.5 us
    unnamed x7, local copies, waits for them, and re-layouts  13.9 us

profile of v1, /device:TPU:12, one launch (start us, length us, event | category | flops | bytes accessed | tf_op | source)
XLA Modules:
  0.0 103.5 jit_solution(9903182476992746852)
XLA Ops:
  0.6 0.1 pad.13.clone
  0.7 0.7 fusion
  1.5 0.1 copy.18
  1.5 0.1 copy.17
  1.6 0.1 pad_maximum_fusion.1
  1.7 0.1 copy.10
  1.8 0.1 copy.13
  1.9 0.1 maximum_bitcast_fusion
  2.1 1.0 copy.22
  3.1 1.0 copy.23
  4.1 1.2 %copy.21 = f32[16,8,4,384]{3,1,2,0:T(8,128)S(1)} copy(f32[16,8,4,384]{3,2,1,0:T(4,128)} %bitcast.27) | data formatting | bytes 1572864
  5.3 9.8 %copy.20 = bf16[192,8,2,1536]{3,1,2,0:T(8,128)(2,1)} copy(bf16[192,8,2,1536]{3,2,1,0:T(2,128)(2,1)} %bitcast.26) | data formatting | bytes 18874368
  15.1 86.5 %shard_map.68 = (f32[128,1536]{1,0:T(8,128)S(1)}, f32[128,128]{1,0:T(8,128)S(1)}) custom-call(bf16[1536,3072]{1,0:T(8,128)(2,1)} %bitcast.25, f32[128,1536]{1,0:T(8,128)S(1)} %bitcast.21, f32[64,1536]{1,0:T(8,128)S(1)} %bitcast.22, f32[64,1536]{1,0:T(8,128)S(1)} %bitcast.23, f32[2,128,128]{2,1,0:T(8,128)S(1)} %pad_maximum_fusion.inv_ref), custom_call_target="tpu_custom_call" | custom-call | tf_op jit(solution)/shard_map/pallas_call | solution.py:335
  101.7 1.1 %reshape.26 = f32[1,1,2,64,4,384]{5,4,3,2,1,0:T(4,128)} reshape(f32[128,1536]{1,0:T(8,128)S(1)} %get-tuple-element.4) | data formatting | bytes 1572864 | tf_op jit(solution)/shard_map/reshape | solution.py:368
  102.8 0.7 copy.19
  (3 shorter events, 0.0 us)

commit v2 on v1

--- a/solution.py
+++ b/solution.py
@@ -36,7 +36,7 @@
     wts, part, xs, rowsum, ys,
     side_send, side_recv, diag_send, diag_recv,
     wside_send, wside_recv, wdiag_send, wdiag_recv,
-    x_send, x_recv, y_send, y_recv,
+    x_send, x_recv, y_send, y_recv, inv_full,
 ):
     rows, k = src_ref.shape
     side = k // 4
@@ -208,10 +208,11 @@
         lane = lax.broadcasted_iota(jnp.int32, (half, LANES), 1)
         low = lane < 2 * nc
         t = jnp.concatenate([jnp.where(low, t, 0.0), jnp.where(low, 0.0, t)], axis=0)
-        c_re = jnp.dot(t, inv_ref[0], preferred_element_type=F32, precision=PRECISE)
-        c_im = jnp.dot(t, inv_ref[1], preferred_element_type=F32, precision=PRECISE)
+        c_re = jnp.dot(t, inv_full[0], preferred_element_type=F32, precision=PRECISE)
+        c_im = jnp.dot(t, inv_full[1], preferred_element_type=F32, precision=PRECISE)
         c = jnp.concatenate([c_re, c_im], axis=0)
-        coef_ref[...] = c
+        coef_ref[0] = c_re[:, :nc]
+        coef_ref[1] = c_im[:, :nc]
         hi, lo = split(c)
         lane = lax.broadcasted_iota(jnp.int32, (rows, LANES), 1)
         mid = (lane >= nc) & (lane < 2 * nc)
@@ -227,6 +228,12 @@
     pack_corners(src_ref, cbuf.at[0], 1.0)
     each(diag, "start")
     each(flat, "start")
+
+    cr, ci = inv_ref[0], inv_ref[1]
+    blank = jnp.zeros((nc, LANES - 3 * nc), F32)
+    for i, (top, bottom) in enumerate(((cr, -ci), (ci, cr))):
+        for j, v in enumerate((top, bottom, top, bottom)):
+            inv_full[i, j * nc:(j + 1) * nc] = jnp.concatenate([v, v, v, blank], axis=1)
 
     lift_hi, lift_lo = split(lift_ref[...])
     lhs[...] = jnp.concatenate([lift_hi, lift_lo], axis=0)
@@ -321,14 +328,6 @@
     src = source_trace.reshape(rows, k)
     rest = restriction.reshape(2 * nc, k)
     lift = prolongation.reshape(2 * nc, k)
-    cr, ci = coarse_inverse[0], coarse_inverse[1]
-
-    def spread(top, bottom):
-        column = jnp.concatenate([top, bottom, top, bottom], axis=0)
-        blank = jnp.zeros((4 * nc, LANES - 3 * nc), F32)
-        return jnp.concatenate([column, column, column, blank], axis=1)
-
-    inv = jnp.stack([spread(cr, -ci), spread(ci, cr)])
     half = nsrc // 2
     dma = pltpu.SemaphoreType.DMA
     vmem = pl.BlockSpec(memory_space=pltpu.VMEM)
@@ -336,7 +335,7 @@
         functools.partial(sweep_kernel, ny, nx, ITERS),
         out_shape=(
             jax.ShapeDtypeStruct((rows, k), F32),
-            jax.ShapeDtypeStruct((rows, LANES), F32),
+            jax.ShapeDtypeStruct((2, nsrc, nc), F32),
         ),
         in_specs=[vmem] * 5,
         out_specs=(vmem, vmem),
@@ -359,14 +358,15 @@
             dma((2, 4)), dma((2, 4)), dma((2, 4)), dma((2, 4)),
             dma((4,)), dma((4,)), dma((4,)), dma((4,)),
             dma((2, nx)), dma((2, nx)), dma((2, ny)), dma((2, ny)),
+            pltpu.VMEM((2, 4 * nc, LANES), F32),
         ],
         compiler_params=pltpu.CompilerParams(
             has_side_effects=True, vmem_limit_bytes=48 * 1024 * 1024
         ),
-    )(table, src, rest, lift, inv)
+    )(table, src, rest, lift, coarse_inverse)
     return (
         traces.reshape(source_trace.shape),
-        coef.reshape(2, nsrc, LANES)[:, :, :nc],
+        coef,
     )
 
 

time: 105 us -> 103 us (0.981)
  local copies, waits for them, and re-layouts: 16 us -> 14.9 us
where the time goes in v2:
time: 103 us; the launch traced here: 102 us
  Pallas kernels  86.5 us (84%)
  local copies, waits for them, and re-layouts  14.9 us (14%)
    pallas_call x1, Pallas kernels, per_device(): pl.pallas_call(functools.partial(sweep_kernel, ny, nx, ITERS), out_shape=...  86.5 us
    unnamed x7, local copies, waits for them, and re-layouts  13.7 us

profile of v2, /device:TPU:12, one launch (start us, length us, event | category | flops | bytes accessed | tf_op | source)
XLA Modules:
  0.0 102.0 jit_solution(11126910502037566980)
XLA Ops:
  0.6 1.0 %copy.10 = f32[8,8,4,384]{3,1,2,0:T(8,128)S(1)} copy(f32[8,8,4,384]{3,2,1,0:T(4,128)} %bitcast.18) | data formatting | bytes 786432
  1.7 1.0 %copy.11 = f32[8,8,4,384]{3,1,2,0:T(8,128)S(1)} copy(f32[8,8,4,384]{3,2,1,0:T(4,128)} %bitcast.19) | data formatting | bytes 786432
  2.7 1.2 %copy.9 = f32[16,8,4,384]{3,1,2,0:T(8,128)S(1)} copy(f32[16,8,4,384]{3,2,1,0:T(4,128)} %bitcast.17) | data formatting | bytes 1572864
  3.9 0.0 copy-start
  3.9 9.8 %copy.8 = bf16[192,8,2,1536]{3,1,2,0:T(8,128)(2,1)} copy(bf16[192,8,2,1536]{3,2,1,0:T(2,128)(2,1)} %bitcast.16) | data formatting | bytes 18874368
  13.7 0.0 copy-done
  13.7 86.5 %shard_map.68 = (f32[128,1536]{1,0:T(8,128)S(1)}, f32[2,64,32]{2,1,0:T(8,128)S(1)}) custom-call(bf16[1536,3072]{1,0:T(8,128)(2,1)} %bitcast.15, f32[128,1536]{1,0:T(8,128)S(1)} %bitcast.12, f32[64,1536]{1,0:T(8,128)S(1)} %bitcast.13, f32[64,1536]{1,0:T(8,128)S(1)} %bitcast.14, f32[2,32,32]{2,1,0:T(8,128)S(1)} %copy-done), custom_call_target="tpu_custom_call" | custom-call | tf_op jit(solution)/shard_map/pallas_call | solution.py:334
  100.2 1.1 %reshape.23 = f32[1,1,2,64,4,384]{5,4,3,2,1,0:T(4,128)} reshape(f32[128,1536]{1,0:T(8,128)S(1)} %get-tuple-element.4) | data formatting | bytes 1572864 | tf_op jit(solution)/shard_map/reshape | solution.py:368
  101.4 0.7 copy.7
Async XLA Ops:
  3.9 9.8 %copy-start = (f32[2,32,32]{2,1,0:T(8,128)S(1)}, f32[2,32,32]{2,1,0:T(8,128)}, u32[]{:S(2)}) copy-start(f32[2,32,32]{2,1,0:T(8,128)} %inv_ref.1) | copy-start | bytes 24580

commit v3 on v2

--- a/solution.py
+++ b/solution.py
@@ -293,14 +293,11 @@
         pack_corners(out, cbuf.at[new], 1.0)
         each(diag, "start")
 
+        each(flat, "start")
+
         @pl.when(it < iters - 1)
         def _():
             restrict_start(new, out)
-
-        each(flat, "start")
-
-        @pl.when(it < iters - 1)
-        def _():
             restrict_turn(new)
 
         return carry

time: 103 us -> 101 us (0.981)
  Pallas kernels: 86.5 us -> 85.4 us
    pallas_call x1, Pallas kernels: 86.5 us -> 85.4 us  [per_device(): pl.pallas_call(functools.partial(sweep_kernel, ny, nx, ITERS), out_shape=...]
where the time goes in v3:
time: 101 us
  Pallas kernels  85.4 us (85%)
  local copies, waits for them, and re-layouts  14.9 us (15%)
    pallas_call x1, Pallas kernels, per_device(): pl.pallas_call(functools.partial(sweep_kernel, ny, nx, ITERS), out_shape=...  85.4 us
    unnamed x7, local copies, waits for them, and re-layouts  13.7 us

profile of v3, /device:TPU:12, one launch (start us, length us, event | category | flops | bytes accessed | tf_op | source)
XLA Modules:
  0.0 100.9 jit_solution(14972240512666868830)
XLA Ops:
  0.6 1.0 %copy.10 = f32[8,8,4,384]{3,1,2,0:T(8,128)S(1)} copy(f32[8,8,4,384]{3,2,1,0:T(4,128)} %bitcast.18) | data formatting | bytes 786432
  1.7 1.0 %copy.11 = f32[8,8,4,384]{3,1,2,0:T(8,128)S(1)} copy(f32[8,8,4,384]{3,2,1,0:T(4,128)} %bitcast.19) | data formatting | bytes 786432
  2.7 1.2 %copy.9 = f32[16,8,4,384]{3,1,2,0:T(8,128)S(1)} copy(f32[16,8,4,384]{3,2,1,0:T(4,128)} %bitcast.17) | data formatting | bytes 1572864
  3.9 0.0 copy-start
  3.9 9.8 %copy.8 = bf16[192,8,2,1536]{3,1,2,0:T(8,128)(2,1)} copy(bf16[192,8,2,1536]{3,2,1,0:T(2,128)(2,1)} %bitcast.16) | data formatting | bytes 18874368
  13.7 0.0 copy-done
  13.7 85.4 %shard_map.68 = (f32[128,1536]{1,0:T(8,128)S(1)}, f32[2,64,32]{2,1,0:T(8,128)S(1)}) custom-call(bf16[1536,3072]{1,0:T(8,128)(2,1)} %bitcast.15, f32[128,1536]{1,0:T(8,128)S(1)} %bitcast.12, f32[64,1536]{1,0:T(8,128)S(1)} %bitcast.13, f32[64,1536]{1,0:T(8,128)S(1)} %bitcast.14, f32[2,32,32]{2,1,0:T(8,128)S(1)} %copy-done), custom_call_target="tpu_custom_call" | custom-call | tf_op jit(solution)/shard_map/pallas_call | solution.py:331
  99.1 1.1 %reshape.23 = f32[1,1,2,64,4,384]{5,4,3,2,1,0:T(4,128)} reshape(f32[128,1536]{1,0:T(8,128)S(1)} %get-tuple-element.4) | data formatting | bytes 1572864 | tf_op jit(solution)/shard_map/reshape | solution.py:365
  100.2 0.7 copy.7
Async XLA Ops:
  3.9 9.8 %copy-start = (f32[2,32,32]{2,1,0:T(8,128)S(1)}, f32[2,32,32]{2,1,0:T(8,128)}, u32[]{:S(2)}) copy-start(f32[2,32,32]{2,1,0:T(8,128)} %inv_ref.1) | copy-start | bytes 24580
